TPU v7x, 32 devices: a whole 2x2x4 slice. The times are simulated.
32 devices in a mesh: orb: 8 (over z, y), clu: 4 (over x, core).
Axes of the slice: x: 2, y: 2, z: 4, core: 2. Of those that a mesh axis runs over, the one named last changes fastest.
Arguments:
- integrals: bfloat16 [1024, 1024, 512], P('orb', 'clu'), may hold values from -1.1953125 to 1.1953125
- metric: bfloat16 [1024, 1024], P(None, 'orb'), may hold values from -0.1875 to 0.1875
- occ_energy: float32 [1024], replicated, may hold values from -2 to -0.5
- virt_energy: float32 [512], replicated, may hold values from 0.5 to 4
- orbital_order: int32 [4, 256], replicated, may hold values from 0 to 255, each once within a row
- pair_first: int32 [4, 8, 4], P('clu', 'orb'), may hold values from 0 to 31
- pair_second: int32 [4, 8, 4], replicated, may hold values from 0 to 255
- pair_live: int32 [4, 8, 4], P('clu', 'orb'), may hold values 0 or 1
Outputs:
- gamma: bfloat16 [1024, 1024, 512], P('orb', 'clu')
Inputs may be any that keep to these rules, and one draw needn't show every extreme that they name: `orbital_order`: each row is a permutation of 0 to 255. `pair_second`: slot s names an orbital of cluster s.
All inputs are finite; a program needn't handle non-finite values. No bound on the sum of `pair_live` on one device may be relied on, other than what follows from the above.
Results may differ from a plain program's by a relative error of at most 0.0052.
Values may be sent and summed in bfloat16 or wider, within the bound.
A program may use at most 256 MiB of HBM per device.

v0:
```python
import functools

import jax
import jax.numpy as jnp
from jax import lax
from jax.experimental import pallas as pl
from jax.experimental.pallas import tpu as pltpu
from jax.sharding import PartitionSpec as P

MESH = pl.DeviceIdType.MESH


def enter(orb, clu):
    barrier = pltpu.get_barrier_semaphore()
    d, c = lax.axis_index("orb"), lax.axis_index("clu")
    me = d * clu + c

    def greet(k, carry):
        to = lax.rem(me + k, orb * clu)
        pl.semaphore_signal(barrier, inc=1, device_id=(to // clu, lax.rem(to, clu)), device_id_type=MESH)
        return carry

    lax.fori_loop(1, orb * clu, greet, 0)
    pl.semaphore_wait(barrier, orb * clu - 1)


def gather_kernel(orb, clu, slots, per, xs, first_ref, second_ref, metric_ref, rows_ref, full_ref,
                  fs, fr, ss, sr, ms, mr, local):
    d, c = lax.axis_index("orb"), lax.axis_index("clu")
    me = d * clu + c
    enter(orb, clu)
    mine = pl.ds(pl.multiple_of(d * xs, xs), xs)

    def first_copy(to, at, sem):
        return pltpu.make_async_remote_copy(
            first_ref.at[to], rows_ref.at[pl.ds(0, slots), at], fs.at[to], fr.at[sem],
            device_id=(to, c), device_id_type=MESH)

    def metric_copy(to, sem):
        return pltpu.make_async_remote_copy(
            metric_ref, full_ref.at[sem], ms.at[to], mr.at[sem], device_id=(to, c), device_id_type=MESH)

    def second_copy(to, at, cluster, sem):
        return pltpu.make_async_remote_copy(
            second_ref.at[to], rows_ref.at[pl.ds(slots + cluster * per, per), at], ss.at[to], sr.at[sem],
            device_id=(to // clu, lax.rem(to, clu)), device_id_type=MESH)

    own = [
        pltpu.make_async_copy(first_ref.at[d], rows_ref.at[pl.ds(0, slots), mine], local.at[0]),
        pltpu.make_async_copy(second_ref.at[me], rows_ref.at[pl.ds(slots + c * per, per), mine], local.at[1]),
        pltpu.make_async_copy(metric_ref, full_ref.at[d], local.at[2]),
    ]
    for copy in own:
        copy.start()

    def start_orb(k, carry):
        to = lax.rem(d + k, orb)
        metric_copy(to, d).start()
        first_copy(to, mine, d).start()
        return carry

    def start_all(k, carry):
        to = lax.rem(me + k, orb * clu)
        second_copy(to, mine, c, me).start()
        return carry

    lax.fori_loop(1, orb, start_orb, 0)
    lax.fori_loop(1, orb * clu, start_all, 0)

    def end_orb(k, carry):
        to = lax.rem(d + k, orb)
        at = pl.ds(pl.multiple_of(to * xs, xs), xs)
        metric_copy(to, to).wait()
        first_copy(to, at, to).wait()
        return carry

    def end_all(k, carry):
        to = lax.rem(me + k, orb * clu)
        at = pl.ds(pl.multiple_of(to // clu * xs, xs), xs)
        second_copy(to, at, lax.rem(to, clu), to).wait()
        return carry

    lax.fori_loop(1, orb, end_orb, 0)
    lax.fori_loop(1, orb * clu, end_all, 0)
    for copy in own:
        copy.wait()


def return_kernel(orb, clu, xs, gamma_ref, back_ref, send, recv, local):
    d, c = lax.axis_index("orb"), lax.axis_index("clu")
    enter(orb, clu)

    def copy_to(to, sem):
        return pltpu.make_async_remote_copy(
            gamma_ref.at[:, pl.ds(pl.multiple_of(to * xs, xs), xs)], back_ref.at[sem], send.at[to], recv.at[sem],
            device_id=(to, c), device_id_type=MESH)

    own = pltpu.make_async_copy(
        gamma_ref.at[:, pl.ds(pl.multiple_of(d * xs, xs), xs)], back_ref.at[d], local.at[0])
    own.start()

    def start(k, carry):
        copy_to(lax.rem(d + k, orb), d).start()
        return carry

    def end(k, carry):
        to = lax.rem(d + k, orb)
        copy_to(to, to).wait()
        return carry

    lax.fori_loop(1, orb, start, 0)
    lax.fori_loop(1, orb, end, 0)
    own.wait()


def on_device(
    integrals, metric, occ_energy, virt_energy, orbital_order, pair_first, pair_second, pair_live
):
    orb, clu = lax.axis_size("orb"), lax.axis_size("clu")
    d, c = lax.axis_index("orb"), lax.axis_index("clu")
    xs, occ, virt = integrals.shape
    aux = metric.shape[0]
    owned = occ // orb
    slots = pair_second.shape[2]
    per = slots // clu
    any_space = pl.BlockSpec(memory_space=pl.ANY)
    dma = pltpu.SemaphoreType.DMA

    own_order = lax.dynamic_index_in_dim(orbital_order, c, 0, keepdims=False)
    all_first = lax.all_gather(pair_first[0, 0], "orb", axis=0, tiled=False)
    first_in = jnp.take_along_axis(own_order.reshape(orb, owned), all_first, axis=1)
    wanted = lax.dynamic_slice_in_dim(pair_second, c * per, per, 2).transpose(1, 0, 2)
    index = jnp.concatenate([first_in.reshape(-1), wanted.reshape(-1)])
    pick = (index[:, None] == jnp.arange(occ, dtype=jnp.int32)[None, :]).astype(jnp.bfloat16)
    picked = jnp.einsum("jo,poa->pja", pick, integrals).transpose(1, 0, 2)
    first_rows = picked[: orb * slots].reshape(orb, slots, xs, virt)
    second_rows = picked[orb * slots :].reshape(orb * clu, per, xs, virt)

    rows, full = pl.pallas_call(
        functools.partial(gather_kernel, orb, clu, slots, per, xs),
        out_shape=[
            jax.ShapeDtypeStruct((2 * slots, aux, virt), jnp.bfloat16),
            jax.ShapeDtypeStruct((orb,) + metric.shape, jnp.bfloat16),
        ],
        in_specs=[any_space] * 3,
        out_specs=[any_space] * 2,
        scratch_shapes=[dma((orb,)), dma((orb,)), dma((orb * clu,)), dma((orb * clu,)), dma((orb,)), dma((orb,)), dma((3,))],
        compiler_params=pltpu.CompilerParams(collective_id=0, has_side_effects=True),
    )(first_rows, second_rows, metric)

    whole_metric = full.transpose(0, 2, 1).reshape(aux, aux)
    fitted = jnp.einsum("qp,spa->sqa", whole_metric, rows, preferred_element_type=jnp.float32).astype(jnp.bfloat16)
    first_fit, second_fit = fitted[:slots], fitted[slots:]
    intersection = jnp.einsum("sqa,sqb->sab", first_fit, second_fit, preferred_element_type=jnp.float32)
    first_slot = pair_first[0, 0]
    live = pair_live[0, 0].astype(jnp.float32)
    first_orb = jnp.take(lax.dynamic_index_in_dim(first_in, d, 0, keepdims=False), jnp.arange(slots)) + c * occ
    own_second = lax.dynamic_index_in_dim(
        lax.dynamic_index_in_dim(pair_second, c, 0, keepdims=False), d, 0, keepdims=False)
    second_orb = own_second + jnp.arange(slots, dtype=jnp.int32) // per * occ
    denominator = (
        virt_energy[None, :, None]
        + virt_energy[None, None, :]
        - occ_energy[first_orb][:, None, None]
        - occ_energy[second_orb][:, None, None]
    )
    amplitude = (live[:, None, None] * intersection / denominator).astype(jnp.bfloat16)
    contribution = jnp.einsum("sab,sqb->sqa", amplitude, second_fit, preferred_element_type=jnp.float32)
    same = first_slot[:, None] == first_slot[None, :]
    gamma = []
    for s in range(slots):
        total = contribution[s]
        for t in range(slots):
            if t != s:
                total = total + jnp.where(same[s, t], contribution[t], 0.0)
        gamma.append(total.astype(jnp.bfloat16))
    gamma = jnp.stack(gamma)

    back = pl.pallas_call(
        functools.partial(return_kernel, orb, clu, xs),
        out_shape=jax.ShapeDtypeStruct((orb, slots, xs, virt), jnp.bfloat16),
        in_specs=[any_space],
        out_specs=any_space,
        scratch_shapes=[dma((orb,)), dma((orb,)), dma((1,))],
        compiler_params=pltpu.CompilerParams(collective_id=1, has_side_effects=True),
    )(gamma)

    earlier = (all_first[:, :, None] == all_first[:, None, :]) & (
        jnp.arange(slots)[None, :, None] > jnp.arange(slots)[None, None, :])
    speaks = ~jnp.any(earlier, axis=2)
    place = (
        (jnp.arange(occ, dtype=jnp.int32)[:, None] == first_in.reshape(-1)[None, :]) & speaks.reshape(-1)[None, :]
    ).astype(jnp.bfloat16)
    back = back.reshape(orb * slots, xs, virt).transpose(1, 0, 2)
    return jnp.einsum("oj,qja->qoa", place, back, preferred_element_type=jnp.float32).astype(jnp.bfloat16)


def solution(mesh):
    in_specs = (
        P("orb", "clu", None),
        P(None, "orb"),
        P(),
        P(),
        P(),
        P("clu", "orb", None),
        P(),
        P("clu", "orb", None),
    )
    out_specs = P("orb", "clu", None)
    return jax.shard_map(
        on_device, mesh=mesh, in_specs=in_specs, out_specs=out_specs, check_vma=False
    )
```

profile of v0, /device:TPU:12, one launch (start us, length us, event | category | flops | bytes accessed | tf_op | source)
XLA Modules:
  0.0 492.4 jit_solution(3461599236508414716)
XLA Ops:
  0.0 0.7 copy-done
  0.7 0.2 dynamic-slice_reduce_fusion
  0.9 0.7 convert_bitcast_fusion.2
  1.5 0.8 broadcast_compare_fusion
  2.4 0.7 dynamic-slice_reduce_fusion.2
  3.3 14.4 %all-gather = s32[8,1,4]{2,1,0:T(1,128)S(1)} all-gather(s32[1,1,4]{2,1,0:T(1,128)} %param.13), channel_id=2, replica_groups=mesh['orb'=8,'clu'=4] {'orb'}, dimensions={0}, use_global_device_ids=true | all-gather | bytes 144 | tf_op jit(solution)/shard_map/all_gather | solution.py:130
  17.8 0.1 and_reduce_fusion
  17.9 0.1 copy.63
  18.0 0.1 not.11
  18.3 0.7 gather_fusion.3
  19.1 0.1 copy.53
  19.2 0.2 dynamic-slice_reduce_fusion.1
  19.3 0.6 gather_fusion
  20.3 0.6 gather_fusion.1
  20.9 0.6 gather_fusion.2
  21.5 0.7 fusion.19
  22.2 0.1 broadcast_add_fusion
  22.4 17.2 %fusion.7 = bf16[64,128,512]{2,0,1:T(8,128)(2,1)} fusion(bf16[128,256,512]{2,1,0:T(8,128)(2,1)} %param.8, s32[64]{0:T(128)S(1)} %pad_add_fusion), kind=kOutput, calls=%fused_computation.20 | convolution fusion | flops 2147500032 | bytes 41943296 | tf_op jit(solution)/shard_map/jo,poa->pja/dot_general | solution.py:135
  39.6 4.0 fusion.18
  43.6 4.3 copy.74
  47.9 4.4 copy.56
  52.3 246.3 %shard_map.82 = (bf16[8,1024,512]{2,1,0:T(8,128)(2,1)}, bf16[8,1024,128]{2,1,0:T(8,128)(2,1)}) custom-call(bf16[8,4,128,512]{3,2,1,0:T(8,128)(2,1)} %bitcast.68, bf16[32,1,128,512]{3,2,1,0:T(8,128)(2,1)} %bitcast.67, bf16[1024,128]{1,0:T(8,128)(2,1)} %metric_ref.1), custom_call_target="tpu_custom_call" | custom-call | tf_op jit(solution)/shard_map/pallas_call | solution.py:139
  298.6 2.9 copy.58
  301.5 11.6 %convert_bitcast_fusion.1 = bf16[8,1024,512]{1,2,0:T(8,128)(2,1)S(1)} fusion(bf16[8,1024,512]{2,1,0:T(8,128)(2,1)} %get-tuple-element.7, bf16[1024,1024,1]{1,0,2:T(8,128)(2,1)S(1)} %bitcast.70), kind=kOutput, calls=%fused_computation.5 | convolution fusion | flops 8594128896 | bytes 18874368 | tf_op jit(solution)/shard_map/qp,spa->sqa/dot_general | solution.py:152
  313.1 2.6 divide_convert_fusion
  315.7 2.8 fusion.20
  318.6 5.2 %add_convert_fusion.1 = (bf16[1,1024,512]{2,1,0:T(8,128)(2,1)S(1)}, bf16[1,1024,512]{2,1,0:T(8,128)(2,1)S(1)}) fusion(f32[4,1024,512]{2,1,0:T(8,128)S(1)} %fusion.20, pred[]{:T(512)} %bitcast.23, pred[]{:T(512)} %bitcast.22, pred[]{:T(512)} %bitcast.21, pred[]{:T(512)} %bitcast.26, pred[]{:T(512)} %bitcast.25, pred[]{:T(512)} %bitcast.24), kind=kLoop, calls=%fused_computation.14 | loop fusion | flops 7340032 | bytes 10485766 | tf_op jit(solution)/shard_map/convert_element_type | solution.py:176
  323.7 5.0 %add_convert_fusion.3 = (bf16[1,1024,512]{2,1,0:T(8,128)(2,1)S(1)}, bf16[1,1024,512]{2,1,0:T(8,128)(2,1)S(1)}) fusion(f32[4,1024,512]{2,1,0:T(8,128)S(1)} %fusion.20, pred[]{:T(512)} %bitcast.17, pred[]{:T(512)} %bitcast.16, pred[]{:T(512)} %bitcast.15, pred[]{:T(512)} %bitcast.20, pred[]{:T(512)} %bitcast.19, pred[]{:T(512)} %bitcast.18), kind=kLoop, calls=%fused_computation.16 | loop fusion | flops 7340032 | bytes 10485766 | tf_op jit(solution)/shard_map/convert_element_type | solution.py:176
  328.7 2.3 pad_maximum_fusion.gamma_ref
  331.0 101.3 %shard_map.83 = bf16[8,4,128,512]{3,2,1,0:T(8,128)(2,1)} custom-call(bf16[4,1024,512]{2,1,0:T(8,128)(2,1)} %pad_maximum_fusion.gamma_ref), custom_call_target="tpu_custom_call" | custom-call | tf_op jit(solution)/shard_map/pallas_call | solution.py:179
  432.3 16.2 %convert_bitcast_fusion = bf16[128,256,512]{1,2,0:T(8,128)(2,1)} fusion(bf16[32,128,512]{2,1,0:T(8,128)(2,1)} %bitcast.66, s32[32]{0:T(128)S(1)} %select_n.158, pred[32]{0:T(512)(128)(4,1)S(1)} %not.11), kind=kOutput, calls=%fused_computation.4 | convolution fusion | flops 1090535424 | bytes 37748896 | tf_op jit(solution)/shard_map/oj,qja->qoa/dot_general | solution.py:195
  448.5 44.0 %copy.64 = bf16[128,256,512]{2,1,0:T(8,128)(2,1)} copy(bf16[128,256,512]{1,2,0:T(8,128)(2,1)} %convert_bitcast_fusion) | data formatting | bytes 67108864 | tf_op jit(solution)/shard_map/convert_element_type | solution.py:195
  (27 shorter events, 0.9 us)
Async XLA Ops:
  0.0 0.7 copy-start
  0.0 20.3 %copy-start.2 = (f32[1024]{0:T(1024)S(1)}, f32[1024]{0:T(1024)}, u32[]{:S(2)}) copy-start(f32[1024]{0:T(1024)} %param.10) | copy-start | bytes 12292
  0.0 22.2 %copy-start.3 = (f32[512]{0:T(512)S(1)}, f32[512]{0:T(512)}, u32[]{:S(2)}) copy-start(f32[512]{0:T(512)} %param.11) | copy-start | bytes 6148
  448.5 44.0 %copy-start.1 = (s32[4,8,4]{1,2,0:T(4,128)S(1)}, s32[4,8,4]{1,2,0:T(4,128)}, u32[]{:S(2)}) copy-start(s32[4,8,4]{1,2,0:T(4,128)} %param.14) | copy-start | bytes 1540
where the time goes:
time: 494 us; the launch traced here: 492 us
  Pallas kernels  348 us (70%)
  local copies, waits for them, and re-layouts  65.6 us (13%)
  matrix products  50.4 us (10%)
  blocking collectives  14.4 us (3%)
  other arithmetic  14.3 us (3%)
    pallas_call x1, Pallas kernels, on_device(): pl.pallas_call(functools.partial(gather_kernel, orb, clu, slots, per, xs)...  246 us
    pallas_call x1, Pallas kernels, on_device(): pl.pallas_call(functools.partial(return_kernel, orb, clu, xs), out_shape=...  101 us
    convert_element_type x1, local copies, waits for them, and re-layouts, on_device(): jnp.einsum('oj,qja->qoa', place, back, preferred_element_type=jnp.float32)  44 us
    dot_general x1, matrix products, on_device(): picked = jnp.einsum('jo,poa->pja', pick, integrals).transpose(1, 0, 2)  17.2 us
    dot_general x1, matrix products, on_device(): jnp.einsum('oj,qja->qoa', place, back, preferred_element_type=jnp.float32)  16.2 us
    all_gather x1, blocking collectives, on_device(): all_first = lax.all_gather(pair_first[0, 0], 'orb', axis=0, tiled=False)  14.4 us
    dot_general x1, matrix products, on_device(): jnp.einsum('qp,spa->sqa', whole_metric, rows, preferred_element_type=jnp....  11.6 us
    convert_element_type x2, other arithmetic, on_device(): gamma.append(total.astype(jnp.bfloat16))  10.1 us

commit v1 on v0

v1 whole, which is shorter than its diff:
```python
import functools

import jax
import jax.numpy as jnp
from jax import lax
from jax.experimental import pallas as pl
from jax.experimental.pallas import tpu as pltpu
from jax.sharding import PartitionSpec as P

MESH = pl.DeviceIdType.MESH
F32 = jnp.float32
BF16 = jnp.bfloat16


def enter(orb, clu):
    barrier = pltpu.get_barrier_semaphore()
    d, c = lax.axis_index("orb"), lax.axis_index("clu")
    me = d * clu + c

    def greet(k, carry):
        to = lax.rem(me + k, orb * clu)
        pl.semaphore_signal(barrier, inc=1, device_id=(to // clu, lax.rem(to, clu)), device_id_type=MESH)
        return carry

    lax.fori_loop(1, orb * clu, greet, 0)
    pl.semaphore_wait(barrier, orb * clu - 1)


def pick_kernel(rows, block, pick_ref, x_ref, out_ref, wide):
    virt = x_ref.shape[2]
    for p in range(block):
        got = jnp.dot(pick_ref[...], x_ref[p], preferred_element_type=F32)
        for lane in range(0, virt, 128):
            wide[lane // 128, pl.ds(p, rows, stride=block), :] = got[:, lane : lane + 128]
    for lane in range(0, virt, 128):
        out_ref[:, :, lane : lane + 128] = wide[lane // 128].reshape(rows, block, 128).astype(BF16)


def place_kernel(rows, block, place_ref, back_ref, out_ref, wide):
    virt = out_ref.shape[2]
    for lane in range(0, virt, 128):
        wide[lane // 128] = back_ref[:, :, lane : lane + 128].astype(F32).reshape(rows * block, 128)
    for q in range(block):
        row = jnp.concatenate(
            [wide[lane // 128, pl.ds(q, rows, stride=block), :] for lane in range(0, virt, 128)], axis=1).astype(BF16)
        out_ref[q] = jnp.dot(place_ref[...], row, preferred_element_type=F32).astype(BF16)


def exchange_kernel(orb, clu, per, xs, table, ve_row, ve_col, picked_ref, mt_ref, back_ref,
                    rows_i, rows_j, mt, fit_i, fit_j, amp, contrib, out,
                    recv_i, recv_j, send_i, send_j, send_j0, recv_back, send_back, m1_send, m1_recv, m2_send, m2_recv):
    d, c = lax.axis_index("orb"), lax.axis_index("clu")
    aux, virt = rows_i.shape[1:]
    slots = clu * per
    width = aux // clu
    chunk = min(256, aux)
    half = min(256, virt)
    mine = pl.ds(pl.multiple_of(d * xs, xs), xs)

    def columns(cluster):
        return pl.ds(pl.multiple_of(cluster * width, width), width)

    def slot_of(t):
        return lax.rem(c + t // per, clu) * per + lax.rem(t, per)

    def second_row(to, cluster, t):
        return picked_ref.at[orb * slots + (to * clu + cluster) * per + lax.rem(t, per)]

    def wait_bytes(ref, sem):
        pltpu.make_async_copy(ref, ref, sem).wait()

    def start_step(t):
        k = t // per
        slot = slot_of(t)
        other = lax.rem(c - k + clu, clu)
        pltpu.make_async_copy(picked_ref.at[d * slots + slot], rows_i.at[t, mine], recv_i.at[t]).start()

        def second(to, sem):
            return pltpu.make_async_remote_copy(
                second_row(to, other, t), rows_j.at[t, mine], sem, recv_j.at[t],
                device_id=(to, other), device_id_type=MESH)

        @pl.when(k == 0)
        def _():
            pltpu.make_async_copy(
                second_row(d, c, t), rows_j.at[t, mine], recv_j.at[t]).start()

        def send(i, carry):
            to = lax.rem(d + i, orb)
            pltpu.make_async_remote_copy(
                picked_ref.at[to * slots + slot], rows_i.at[t, mine], send_i.at[t], recv_i.at[t],
                device_id=(to, c), device_id_type=MESH).start()
            second(to, send_j.at[t]).start()
            return carry

        lax.fori_loop(1, orb, send, 0)

        @pl.when(k != 0)
        def _():
            second(d, send_j0.at[t]).start()

    enter(orb, clu)

    pltpu.make_async_copy(mt_ref.at[:, columns(c)], mt.at[mine, columns(c)], m1_recv.at[0]).start()

    def send_metric(i, carry):
        to = lax.rem(d + i, orb)
        pltpu.make_async_remote_copy(
            mt_ref.at[:, columns(c)], mt.at[mine, columns(c)], m1_send.at[0], m1_recv.at[0],
            device_id=(to, c), device_id_type=MESH).start()
        return carry

    lax.fori_loop(1, orb, send_metric, 0)
    start_step(jnp.int32(0))
    if slots > 1:
        start_step(jnp.int32(1))

    wait_bytes(mt.at[:, columns(c)], m1_recv.at[0])

    def share(cluster, sem):
        return pltpu.make_async_remote_copy(
            mt.at[:, columns(c)], mt.at[:, columns(c)], m2_send.at[cluster], m2_recv.at[sem],
            device_id=(d, cluster), device_id_type=MESH)

    for i in range(1, clu):
        share(lax.rem(c + i, clu), c).start()
    for i in range(1, clu):
        cluster = lax.rem(c + i, clu)
        wait_bytes(mt.at[:, columns(cluster)], m2_recv.at[cluster])

    def step(t, carry):
        slot = slot_of(t)
        wait_bytes(rows_i.at[t], recv_i.at[t])
        wait_bytes(rows_j.at[t], recv_j.at[t])

        @pl.when(t + 2 < slots)
        def _():
            start_step(t + 2)

        def fit(i, carry):
            at = pl.ds(pl.multiple_of(i * chunk, chunk), chunk)
            left = mt[at, :]
            fit_i[at, :] = jnp.dot(left, rows_i[t], preferred_element_type=F32).astype(BF16)
            fit_j[at, :] = jnp.dot(left, rows_j[t], preferred_element_type=F32).astype(BF16)
            return carry

        lax.fori_loop(0, aux // chunk, fit, 0)

        live, occ_i, occ_j = table[slot, 0], table[slot, 1], table[slot, 2]
        for a in range(0, virt, half):
            cross = lax.dot_general(
                fit_i[:, a : a + half], fit_j[...], (((0,), (0,)), ((), ())), preferred_element_type=F32)
            gap = ve_col[a : a + half, :] + ve_row[...] - occ_i - occ_j
            amp[a : a + half, :] = (live * cross / gap).astype(BF16)

        def gamma(i, carry):
            at = pl.ds(pl.multiple_of(i * chunk, chunk), chunk)
            own = lax.dot_general(
                fit_j[at, :], amp[...], (((1,), (1,)), ((), ())), preferred_element_type=F32)
            contrib[t, at, :] = own

            def add(u, total):
                return total + table[slot, 3 + slot_of(u)] * contrib[u, at, :]

            out[t, at, :] = lax.fori_loop(0, t, add, own).astype(BF16)
            return carry

        lax.fori_loop(0, aux // chunk, gamma, 0)

        pltpu.make_async_copy(out.at[t, mine], back_ref.at[d, slot], recv_back.at[t]).start()

        def send_back_to(i, carry):
            to = lax.rem(d + i, orb)
            pltpu.make_async_remote_copy(
                out.at[t, pl.ds(pl.multiple_of(to * xs, xs), xs)], back_ref.at[d, slot],
                send_back.at[t], recv_back.at[t], device_id=(to, c), device_id_type=MESH).start()
            return carry

        lax.fori_loop(1, orb, send_back_to, 0)
        return carry

    lax.fori_loop(0, slots, step, 0)

    others = pl.ds(0, (orb - 1) * xs)
    wait_bytes(mt.at[pl.ds(0, (orb - 1) * xs), columns(c)], m1_send.at[0])
    for i in range(1, clu):
        wait_bytes(mt.at[:, columns(c)], m2_send.at[lax.rem(c + i, clu)])

    def finish(t, carry):
        wait_bytes(rows_i.at[t, others], send_i.at[t])
        wait_bytes(rows_j.at[t, others], send_j.at[t])

        @pl.when(t // per != 0)
        def _():
            wait_bytes(rows_j.at[t, mine], send_j0.at[t])

        wait_bytes(out.at[t, others], send_back.at[t])
        wait_bytes(out.at[t], recv_back.at[t])
        return carry

    lax.fori_loop(0, slots, finish, 0)


def on_device(
    integrals, metric, occ_energy, virt_energy, orbital_order, pair_first, pair_second, pair_live
):
    orb, clu = lax.axis_size("orb"), lax.axis_size("clu")
    d, c = lax.axis_index("orb"), lax.axis_index("clu")
    xs, occ, virt = integrals.shape
    aux = metric.shape[0]
    owned = occ // orb
    slots = pair_second.shape[2]
    per = slots // clu
    any_space = pl.BlockSpec(memory_space=pl.ANY)
    vmem = pl.BlockSpec(memory_space=pltpu.VMEM)
    dma = pltpu.SemaphoreType.DMA

    own_order = lax.dynamic_index_in_dim(orbital_order, c, 0, keepdims=False)
    first_slot = pair_first[0, 0]
    all_first = lax.all_gather(first_slot, "orb", axis=0, tiled=False)
    first_in = jnp.take_along_axis(own_order.reshape(orb, owned), all_first, axis=1)
    wanted = lax.dynamic_slice_in_dim(pair_second, c * per, per, 2).transpose(1, 0, 2)
    index = jnp.concatenate([first_in.reshape(-1), wanted.reshape(-1)])
    numbers = jnp.arange(occ, dtype=jnp.int32)
    pick = (index[:, None] == numbers[None, :]).astype(BF16)
    count = index.shape[0]
    block = min(16, xs)
    picked = pl.pallas_call(
        functools.partial(pick_kernel, count, block),
        grid=(xs // block,),
        out_shape=jax.ShapeDtypeStruct((count, xs, virt), BF16),
        in_specs=[
            pl.BlockSpec((count, occ), lambda i: (0, 0)),
            pl.BlockSpec((block, occ, virt), lambda i: (i, 0, 0)),
        ],
        out_specs=pl.BlockSpec((count, block, virt), lambda i: (0, i, 0)),
        scratch_shapes=[pltpu.VMEM((virt // 128, count * block, 128), F32)],
    )(pick, integrals)

    live = pair_live[0, 0].astype(F32)
    first_orb = lax.dynamic_index_in_dim(first_in, d, 0, keepdims=False) + c * occ
    own_second = lax.dynamic_index_in_dim(
        lax.dynamic_index_in_dim(pair_second, c, 0, keepdims=False), d, 0, keepdims=False)
    second_orb = own_second + jnp.arange(slots, dtype=jnp.int32) // per * occ
    same = (first_slot[:, None] == first_slot[None, :]).astype(F32)
    table = jnp.concatenate(
        [jnp.stack([live, occ_energy[first_orb], occ_energy[second_orb]], axis=1), same], axis=1)

    back = pl.pallas_call(
        functools.partial(exchange_kernel, orb, clu, per, xs),
        out_shape=jax.ShapeDtypeStruct((orb, slots, xs, virt), BF16),
        in_specs=[pl.BlockSpec(memory_space=pltpu.SMEM), vmem, vmem, any_space, any_space],
        out_specs=any_space,
        scratch_shapes=[
            pltpu.VMEM((slots, aux, virt), BF16),
            pltpu.VMEM((slots, aux, virt), BF16),
            pltpu.VMEM((aux, aux), BF16),
            pltpu.VMEM((aux, virt), BF16),
            pltpu.VMEM((aux, virt), BF16),
            pltpu.VMEM((virt, virt), BF16),
            pltpu.VMEM((slots, aux, virt), F32),
            pltpu.VMEM((slots, aux, virt), BF16),
        ] + [dma((slots,))] * 7 + [dma((1,)), dma((1,)), dma((clu,)), dma((clu,))],
        compiler_params=pltpu.CompilerParams(collective_id=0, has_side_effects=True),
    )(table, virt_energy[None, :], virt_energy[:, None], picked, metric.T)

    order = lax.rem(jnp.arange(slots, dtype=jnp.int32) // per - c + clu, clu) * per + jnp.arange(slots) % per
    later = (all_first[:, :, None] == all_first[:, None, :]) & (order[None, None, :] > order[None, :, None])
    speaks = ~jnp.any(later, axis=2)
    place = ((numbers[:, None] == first_in.reshape(-1)[None, :]) & speaks.reshape(-1)[None, :]).astype(BF16)
    count = orb * slots
    return pl.pallas_call(
        functools.partial(place_kernel, count, block),
        grid=(xs // block,),
        out_shape=jax.ShapeDtypeStruct((xs, occ, virt), BF16),
        in_specs=[
            pl.BlockSpec((occ, count), lambda i: (0, 0)),
            pl.BlockSpec((count, block, virt), lambda i: (0, i, 0)),
        ],
        out_specs=pl.BlockSpec((block, occ, virt), lambda i: (i, 0, 0)),
        scratch_shapes=[pltpu.VMEM((virt // 128, count * block, 128), F32)],
    )(place, back.reshape(count, xs, virt))


def solution(mesh):
    in_specs = (
        P("orb", "clu", None),
        P(None, "orb"),
        P(),
        P(),
        P(),
        P("clu", "orb", None),
        P(),
        P("clu", "orb", None),
    )
    out_specs = P("orb", "clu", None)
    return jax.shard_map(
        on_device, mesh=mesh, in_specs=in_specs, out_specs=out_specs, check_vma=False
    )
```

time: 494 us -> 363 us (0.73)
  local copies, waits for them, and re-layouts: 65.6 us -> 9.52 us
  matrix products: 50.4 us -> 0 us
  Pallas kernels: 348 us -> 331 us
  other arithmetic: 14.3 us -> 3.92 us
    dot_general x5 -> x0, matrix products: 50.4 us -> none  [the longest x1 17.2 us: on_device(): picked = jnp.einsum('jo,poa->pja', pick, integrals).transpose(1, 0, 2)]
    convert_element_type x1, local copies, waits for them, and re-layouts: 44 us -> 0.09 us  [on_device(): live = pair_live[0, 0].astype(F32)]
    pallas_call x2 -> x3, Pallas kernels: 348 us -> 331 us  [the longest x1 296 us: on_device(): pl.pallas_call(functools.partial(exchange_kernel, orb, clu, per, xs), out...]
    slice x3 -> x0, local copies, waits for them, and re-layouts: 9.05 us -> none  [the longest x1 4.36 us: on_device(): first_rows = picked[:orb * slots].reshape(orb, slots, xs, virt)]
    convert_element_type x3 -> x4, other arithmetic: 10.8 us -> 2.78 us  [the longest x1 0.8 us: on_device(): same = (first_slot[:, None] == first_slot[None, :]).astype(F32)]
where the time goes in v1:
time: 363 us; the launch traced here: 359 us
  Pallas kernels  331 us (91%)
  blocking collectives  14.4 us (4%)
  local copies, waits for them, and re-layouts  9.52 us (3%)
  other arithmetic  3.92 us (1%)
    pallas_call x1, Pallas kernels, on_device(): pl.pallas_call(functools.partial(exchange_kernel, orb, clu, per, xs), out...  296 us
    pallas_call x1, Pallas kernels, on_device(): pl.pallas_call(functools.partial(pick_kernel, count, block), grid=(xs //...  19.7 us
    pallas_call x1, Pallas kernels, on_device(): pl.pallas_call(functools.partial(place_kernel, count, block), grid=(xs //...  15.7 us
    all_gather x1, blocking collectives, on_device(): all_first = lax.all_gather(first_slot, 'orb', axis=0, tiled=False)  14.4 us

profile of v1, /device:TPU:12, one launch (start us, length us, event | category | flops | bytes accessed | tf_op | source)
XLA Modules:
  0.0 359.4 jit_solution(6975946599171539313)
XLA Ops:
  0.0 0.7 copy-done
  0.7 0.2 dynamic-slice_reduce_fusion
  1.0 0.7 convert_bitcast_fusion
  1.6 0.7 dynamic-slice_reduce_fusion.1
  2.3 0.1 copy.49
  2.4 0.1 copy.52
  2.5 0.1 reshape.162
  2.6 0.8 compare_convert_fusion
  3.5 14.4 %all-gather = s32[8,1,4]{2,1,0:T(1,128)S(1)} all-gather(s32[1,1,4]{2,1,0:T(1,128)} %param.13), channel_id=2, replica_groups=mesh['orb'=8,'clu'=4] {'orb'}, dimensions={0}, use_global_device_ids=true | all-gather | bytes 144 | tf_op jit(solution)/shard_map/all_gather | solution.py:220
  17.9 0.1 copy.44
  18.0 0.1 and_reduce_fusion
  18.1 0.1 copy.48
  18.2 0.1 not.11
  18.3 0.1 copy.45
  18.4 0.1 reshape.180
  18.5 0.7 gather_fusion.2
  19.2 0.1 copy.46
  19.3 0.2 add_reduce_fusion
  19.5 0.1 copy.47
  19.6 0.1 select_n.71
  19.8 1.3 gather_fusion
  21.1 0.1 copy.50
  21.2 1.3 gather_fusion.1
  22.5 0.1 copy.51
  22.6 0.6 pad_maximum_fusion.table
  23.3 0.7 fusion.2.pick_ref
  23.9 0.6 fusion.1.place_ref
  24.6 1.8 copy.53
  26.4 1.5 copy.54.ve_col
  27.9 19.7 %shard_map.82.picked_ref = bf16[64,128,512]{2,1,0:T(8,128)(2,1)} custom-call(bf16[64,256]{1,0:T(8,128)(2,1)} %fusion.2.pick_ref, bf16[128,256,512]{2,1,0:T(8,128)(2,1)} %x_ref.1), custom_call_target="tpu_custom_call" | custom-call | tf_op jit(solution)/shard_map/pallas_call | solution.py:228
  47.6 296.0 %shard_map.83 = bf16[8,4,128,512]{3,2,1,0:T(8,128)(2,1)} custom-call(f32[4,7]{1,0:T(4,128)} %pad_maximum_fusion.table, f32[1,512]{1,0:T(1,128)} %bitcast.34, f32[512,1]{1,0:T(8,128)} %copy.54.ve_col, bf16[64,128,512]{2,1,0:T(8,128)(2,1)} %shard_map.82.picked_ref, bf16[128,1024]{1,0:T(8,128)(2,1)} %bitcast.31), custom_call_target="tpu_custom_call" | custom-call | tf_op jit(solution)/shard_map/pallas_call | solution.py:249
  343.7 15.7 %shard_map.84 = bf16[128,256,512]{2,1,0:T(8,128)(2,1)} custom-call(bf16[256,32]{1,0:T(8,128)(2,1)} %fusion.1.place_ref, bf16[32,128,512]{2,1,0:T(8,128)(2,1)} %bitcast.30), custom_call_target="tpu_custom_call" | custom-call | tf_op jit(solution)/shard_map/pallas_call | solution.py:272
  (15 shorter events, 0.4 us)
Async XLA Ops:
  0.0 0.7 copy-start
  27.9 331.5 %copy-start.1 = (s32[4,8,4]{1,2,0:T(4,128)S(1)}, s32[4,8,4]{1,2,0:T(4,128)}, u32[]{:S(2)}) copy-start(s32[4,8,4]{1,2,0:T(4,128)} %param.14) | copy-start | bytes 1540
